TPU v7x, 32 devices: a whole 2x2x4 slice. The times are simulated.
32 devices in a mesh: ga: 8 (over z, y), ba: 4 (over x, core).
Axes of the slice: x: 2, y: 2, z: 4, core: 2. Of those that a mesh axis runs over, the one named last changes fastest.
Arguments:
- coefficients: bfloat16 [10240, 6144], P('ga', 'ba')
- rotation: bfloat16 [6144, 6144], P('ga', 'ba'), may hold values from -0.078125 to 0.078125
Outputs:
- new_coefficients: bfloat16 [10240, 6144], P('ga', 'ba')
- band_rms: float32 [6144], P('ba')
All inputs are finite; a program needn't handle non-finite values.
Results may differ from a plain program's by a relative error of at most 0.0004.
Values may be sent and summed in bfloat16 or wider, within the bound.
A program may use at most 128 MiB of HBM per device.

v0:
```python
import jax
import jax.numpy as jnp
from jax import lax
from jax.sharding import PartitionSpec as P


def body(coefficients, rotation):
    all_bands = lax.all_gather(coefficients, "ba", axis=1, tiled=True)
    rotated = jnp.dot(
        all_bands,
        lax.all_gather(rotation, "ga", axis=0, tiled=True),
        preferred_element_type=jnp.float32,
    )
    squares = lax.psum(jnp.sum(rotated * rotated, axis=0), "ga")
    total_rows = coefficients.shape[0] * lax.axis_size("ga")
    band_rms = jnp.sqrt(squares / total_rows + 1e-06)
    return ((rotated / band_rms).astype(jnp.bfloat16), band_rms)


def solution(mesh):
    in_specs = (P("ga", "ba"), P("ga", "ba"))
    out_specs = (P("ga", "ba"), P("ba"))
    return jax.shard_map(body, mesh=mesh, in_specs=in_specs, out_specs=out_specs, check_vma=False)
```

profile of v0, /device:TPU:0, one launch (start us, length us, event | category | flops | bytes accessed | tf_op | source)
XLA Modules:
  0.0 543.6 jit_solution(14183646409815637874)
XLA Ops:
  7.2 0.0 all-gather.3.cloned.1.call-start
  7.2 0.7 all-gather.3.cloned.1.call-update
  7.9 0.0 all-gather.5.cloned.1.call-start
  7.9 0.7 all-gather.5.cloned.1.call-update
  8.6 103.6 %all-gather.3.cloned.1.call-done = bf16[1280,6144]{1,0:T(8,128)(2,1)} async-done(((bf16[1280,1536]{1,0:T(8,128)(2,1)}), bf16[1280,6144]{1,0:T(8,128)(2,1)}) %all-gather.3.cloned.1.call-update) | async-done | bytes 15728656 | tf_op jit(solution)/shard_map/all_gather | solution.py:8
  112.2 364.0 %all-gather.5.cloned.1.call-done = bf16[6144,1536]{1,0:T(8,128)(2,1)} async-done(((bf16[768,1536]{1,0:T(8,128)(2,1)}), bf16[6144,1536]{1,0:T(8,128)(2,1)}) %all-gather.5.cloned.1.call-update) | async-done | bytes 18874384 | tf_op jit(solution)/shard_map/all_gather | solution.py:11
  476.2 33.9 %multiply_reduce_fusion = (f32[1536]{0:T(1024)S(1)}, f32[1280,1536]{1,0:T(8,128)}) fusion(bf16[1280,6144]{1,0:T(8,128)(2,1)} %all-gather.3.cloned.1.call-done, bf16[6144,1536]{1,0:T(8,128)(2,1)} %all-gather.5.cloned.1.call-done), kind=kOutput, calls=%fused_computation.1 | convolution fusion | flops 24163121152 | bytes 42473472 | tf_op jit(solution)/shard_map/dot_general | solution.py:9
  510.1 20.4 %psum.7 = f32[1536]{0:T(1024)S(1)} all-reduce(f32[1536]{0:T(1024)S(1)} %get-tuple-element.2), channel_id=1, replica_groups=mesh['ga'=8,'ba'=4] {'ga'}, use_global_device_ids=true, to_apply=%region_1.0 | all-reduce | flops 1536 | bytes 12288 | tf_op jit(solution)/shard_map/psum | solution.py:14
  530.6 0.0 copy-start
  530.6 6.2 %divide_convert_fusion = bf16[1280,1536]{1,0:T(8,128)(2,1)} fusion(f32[1280,1536]{1,0:T(8,128)} %get-tuple-element.3, f32[1536]{0:T(1024)S(1)} %add_sqrt_fusion), kind=kLoop, calls=%fused_computation | loop fusion | flops 3932160 | bytes 11802624 | tf_op jit(solution)/shard_map/convert_element_type | solution.py:17
  536.8 0.0 copy-done
  (1 shorter events, 0.0 us)
Async XLA Ops:
  7.2 105.1 %all-gather.3.cloned.1.call-start = ((), (), s32[]{:S(2)}) async-start(), calls=%async_computation | async-start | bytes 19660800 | tf_op jit(solution)/shard_map/all_gather | solution.py:8
  7.9 468.3 %all-gather.5.cloned.1.call-start = ((), (), s32[]{:S(2)}) async-start(), calls=%async_computation.1 | async-start | bytes 21233664 | tf_op jit(solution)/shard_map/all_gather | solution.py:11
  530.6 6.2 %copy-start = (f32[1536]{0:T(1024)}, f32[1536]{0:T(1024)S(1)}, u32[]{:S(2)}) copy-start(f32[1536]{0:T(1024)S(1)} %add_sqrt_fusion) | copy-start | bytes 18436
Sparse Core Ops, SparseCore 0:
  9.5 102.6 all-gather.2
  113.8 362.3 all-gather.4
where the time goes:
time: 544 us
  waiting for transfers between devices  469 us (86%)
  matrix products  33.9 us (6%)
  blocking collectives  20.4 us (4%)
  between operations  14.1 us (3%)
  other arithmetic  6.19 us (1%)
    all_gather x1, waiting for transfers between devices, body(): lax.all_gather(rotation, 'ga', axis=0, tiled=True)  364 us
    all_gather x1, waiting for transfers between devices, body(): all_bands = lax.all_gather(coefficients, 'ba', axis=1, tiled=True)  104 us
    dot_general x1, matrix products, body(): jnp.dot(all_bands, lax.all_gather(rotation, 'ga', axis=0, tiled=True), pr...  33.9 us
    psum x1, blocking collectives, body(): squares = lax.psum(jnp.sum(rotated * rotated, axis=0), 'ga')  20.4 us
  transfers between devices with their start and end apart: 2, of which 2 were waited for; matrix products, arithmetic and copies ran while one was open for 0% of the time, Pallas kernels for 0%

commit v1 on v0

--- a/solution.py
+++ b/solution.py
@@ -5,7 +5,12 @@
 
 
 def body(coefficients, rotation):
-    all_bands = lax.all_gather(coefficients, "ba", axis=1, tiled=True)
+    ring = [coefficients]
+    for hop in range(3):
+        ring.append(lax.ppermute(ring[-1], "ba", [(dev, (dev + 1) % 4) for dev in range(4)]))
+    all_bands = jnp.roll(
+        jnp.concatenate(ring[::-1], axis=1), (lax.axis_index("ba") + 1) * ring[0].shape[1], axis=1
+    )
     rotated = jnp.dot(
         all_bands,
         lax.all_gather(rotation, "ga", axis=0, tiled=True),

time: 544 us -> 443 us (0.81)
  waiting for transfers between devices: 469 us -> 336 us
  local copies, waits for them, and re-layouts: 0.01 us -> 30.4 us
    all_gather x1, waiting for transfers between devices: 364 us -> 200 us  [body(): lax.all_gather(rotation, 'ga', axis=0, tiled=True)]
    ppermute x0 -> x3, waiting for transfers between devices: none -> 136 us  [body(): lax.ppermute(ring[-1], 'ba', [(dev, (dev + 1) % 4) for dev in range(4)])]
    all_gather x1 -> x0, waiting for transfers between devices: 104 us -> none  [body(): all_bands = lax.all_gather(coefficients, 'ba', axis=1, tiled=True)]
    unnamed x2 -> x15, local copies, waits for them, and re-layouts: 0.01 us -> 28.3 us
  transfers between devices with their start and end apart: 2 -> 4, of which waited for: 2 -> 4; matrix products, arithmetic and copies ran while one was open for 0% -> 6% of each run, Pallas kernels for 0% -> 0%
where the time goes in v1:
time: 443 us; the launch traced here: 442 us
  waiting for transfers between devices  336 us (76%)
  matrix products  34.3 us (8%)
  local copies, waits for them, and re-layouts  30.4 us (7%)
  blocking collectives  20.4 us (5%)
  between operations  14.1 us (3%)
  other arithmetic  6.19 us (1%)
    all_gather x1, waiting for transfers between devices, body(): lax.all_gather(rotation, 'ga', axis=0, tiled=True)  200 us
    ppermute x3, waiting for transfers between devices, body(): lax.ppermute(ring[-1], 'ba', [(dev, (dev + 1) % 4) for dev in range(4)])  136 us
    dot_general x1, matrix products, body(): jnp.dot(all_bands, lax.all_gather(rotation, 'ga', axis=0, tiled=True), pr...  34.3 us
    unnamed x15, local copies, waits for them, and re-layouts  28.3 us
    psum x1, blocking collectives, body(): squares = lax.psum(jnp.sum(rotated * rotated, axis=0), 'ga')  20.4 us
  transfers between devices with their start and end apart: 4, of which 4 were waited for; matrix products, arithmetic and copies ran while one was open for 6% of the time, Pallas kernels for 0%

profile of v1, /device:TPU:0, one launch (start us, length us, event | category | flops | bytes accessed | tf_op | source)
XLA Modules:
  0.0 442.4 jit_solution(8446889258284561667)
XLA Ops:
  7.2 0.0 all-gather.2.cloned.1.call-start
  7.2 0.7 all-gather.2.cloned.1.call-update
  7.9 0.5 collective-permute-start
  8.4 45.5 %collective-permute-done = bf16[1280,1536]{1,0:T(8,128)(2,1)S(1)} collective-permute-done((bf16[1280,1536]{1,0:T(8,128)(2,1)}, bf16[1280,1536]{1,0:T(8,128)(2,1)S(1)}, u32[]{:S(2)}, u32[]{:S(2)}) %collective-permute-start) | collective-permute-done | bytes 3932192 | tf_op jit(solution)/shard_map/ppermute | solution.py:10
  53.9 0.0 copy-start.1
  53.9 1.9 copy-done.1
  55.9 0.0 collective-permute-start.1
  55.9 45.2 %collective-permute-done.1 = bf16[1280,1536]{1,0:T(8,128)(2,1)} collective-permute-done((bf16[1280,1536]{1,0:T(8,128)(2,1)S(1)}, bf16[1280,1536]{1,0:T(8,128)(2,1)}, u32[]{:S(2)}, u32[]{:S(2)}) %collective-permute-start.1) | collective-permute-done | bytes 3932192 | tf_op jit(solution)/shard_map/ppermute | solution.py:10
  101.1 0.0 collective-permute-start.2
  101.1 0.0 copy-start
  101.1 45.4 %collective-permute-done.2 = bf16[1280,1536]{1,0:T(8,128)(2,1)} collective-permute-done((bf16[1280,1536]{1,0:T(8,128)(2,1)}, bf16[1280,1536]{1,0:T(8,128)(2,1)}, u32[]{:S(2)}, u32[]{:S(2)}) %collective-permute-start.2) | collective-permute-done | bytes 3932192 | tf_op jit(solution)/shard_map/ppermute | solution.py:10
  146.5 4.3 constant_dynamic-update-slice_fusion.7
  150.8 0.0 copy-start.2
  150.8 4.5 %constant_dynamic-update-slice_fusion.6 = bf16[1280,12288]{1,0:T(8,128)(2,1)} fusion(bf16[1280,12288]{1,0:T(8,128)(2,1)} %constant_dynamic-update-slice_fusion.7, bf16[1280,1536]{1,0:T(8,128)(2,1)} %collective-permute-done.1), kind=kLoop, calls=%fused_computation.10 | loop fusion | bytes 7864320
  155.3 4.4 constant_dynamic-update-slice_fusion.5
  159.7 0.0 copy-done
  159.7 2.2 constant_dynamic-update-slice_fusion.4
  161.9 4.3 constant_dynamic-update-slice_fusion.3
  166.2 4.4 constant_dynamic-update-slice_fusion.2
  170.7 0.0 copy-done.2
  170.7 2.2 constant_dynamic-update-slice_fusion.1
  172.9 2.2 constant_dynamic-update-slice_fusion
  175.0 199.6 %all-gather.2.cloned.1.call-done = bf16[6144,1536]{1,0:T(8,128)(2,1)} async-done(((bf16[768,1536]{1,0:T(8,128)(2,1)}), bf16[6144,1536]{1,0:T(8,128)(2,1)}) %all-gather.2.cloned.1.call-update) | async-done | bytes 18874384 | tf_op jit(solution)/shard_map/all_gather | solution.py:16
  374.7 34.3 %multiply_reduce_fusion = (f32[1536]{0:T(1024)S(1)}, f32[1280,1536]{1,0:T(8,128)}) fusion(bf16[6144,1536]{1,0:T(8,128)(2,1)} %all-gather.2.cloned.1.call-done, bf16[1280,12288]{1,0:T(8,128)(2,1)} %constant_dynamic-update-slice_fusion, s32[]{:T(128)S(6)} %select_n.14), kind=kOutput, calls=%fused_computation.3 | convolution fusion | flops 24163121152 | bytes 42473476 | tf_op jit(solution)/shard_map/dot_general | solution.py:14
  408.9 20.4 %psum.7 = f32[1536]{0:T(1024)S(1)} all-reduce(f32[1536]{0:T(1024)S(1)} %get-tuple-element.2), channel_id=1, replica_groups=mesh['ga'=8,'ba'=4] {'ga'}, use_global_device_ids=true, to_apply=%region_1.2 | all-reduce | flops 1536 | bytes 12288 | tf_op jit(solution)/shard_map/psum | solution.py:19
  429.4 0.0 copy-start.3
  429.4 6.2 %divide_convert_fusion = bf16[1280,1536]{1,0:T(8,128)(2,1)} fusion(f32[1280,1536]{1,0:T(8,128)} %get-tuple-element.3, f32[1536]{0:T(1024)S(1)} %add_sqrt_fusion), kind=kLoop, calls=%fused_computation.2 | loop fusion | flops 3932160 | bytes 11802624 | tf_op jit(solution)/shard_map/convert_element_type | solution.py:22
  435.6 0.0 copy-done.3
  (1 shorter events, 0.0 us)
Async XLA Ops:
  7.2 367.5 %all-gather.2.cloned.1.call-start = ((), (), s32[]{:S(2)}) async-start(), calls=%async_computation | async-start | bytes 21233664 | tf_op jit(solution)/shard_map/all_gather | solution.py:16
  7.9 46.0 %collective-permute-start = (bf16[1280,1536]{1,0:T(8,128)(2,1)}, bf16[1280,1536]{1,0:T(8,128)(2,1)S(1)}, u32[]{:S(2)}, u32[]{:S(2)}) collective-permute-start(bf16[1280,1536]{1,0:T(8,128)(2,1)} %param.2), channel_id=1, source_target_pairs={{0,1},{1,2},{2,3},{3,0},{4,5},{5,6},{6,7},{7,4},{8,9},{9,10},{10,1... | collective-permute-start | bytes 11796488 | tf_op jit(solution)/shard_map/ppermute | solution.py:10
  53.9 1.9 copy-start.1
  55.9 45.2 %collective-permute-start.1 = (bf16[1280,1536]{1,0:T(8,128)(2,1)S(1)}, bf16[1280,1536]{1,0:T(8,128)(2,1)}, u32[]{:S(2)}, u32[]{:S(2)}) collective-permute-start(bf16[1280,1536]{1,0:T(8,128)(2,1)S(1)} %collective-permute-done), channel_id=1, source_target_pairs={{0,1},{1,2},{2,3},{3,0},{4,5},{5,6},{6,7},{7,4},{8,9},{9,10},{10,1... | collective-permute-start | bytes 11796488 | tf_op jit(solution)/shard_map/ppermute | solution.py:10
  101.1 45.4 %collective-permute-start.2 = (bf16[1280,1536]{1,0:T(8,128)(2,1)}, bf16[1280,1536]{1,0:T(8,128)(2,1)}, u32[]{:S(2)}, u32[]{:S(2)}) collective-permute-start(bf16[1280,1536]{1,0:T(8,128)(2,1)} %collective-permute-done.1), channel_id=1, source_target_pairs={{0,1},{1,2},{2,3},{3,0},{4,5},{5,6},{6,7},{7,4},{8,9},{9,10},{10,1... | collective-permute-start | bytes 11796488 | tf_op jit(solution)/shard_map/ppermute | solution.py:10
  101.1 58.6 %copy-start = (bf16[1280,1536]{1,0:T(8,128)(2,1)S(1)}, bf16[1280,1536]{1,0:T(8,128)(2,1)}, u32[]{:S(2)}) copy-start(bf16[1280,1536]{1,0:T(8,128)(2,1)} %param.2) | copy-start | bytes 11796484
  150.8 19.9 %copy-start.2 = (bf16[1280,1536]{1,0:T(8,128)(2,1)S(1)}, bf16[1280,1536]{1,0:T(8,128)(2,1)}, u32[]{:S(2)}) copy-start(bf16[1280,1536]{1,0:T(8,128)(2,1)} %copy-done.1) | copy-start | bytes 11796484
  429.4 6.2 %copy-start.3 = (f32[1536]{0:T(1024)}, f32[1536]{0:T(1024)S(1)}, u32[]{:S(2)}) copy-start(f32[1536]{0:T(1024)S(1)} %add_sqrt_fusion) | copy-start | bytes 18436
Sparse Core Ops, SparseCore 0:
  9.5 365.1 all-gather.1
